TPU v7x, 32 devices: a whole 2x2x4 slice. The times are simulated.
32 devices in a mesh: facet: 4 (over y, core), team: 4 (over z), sub: 2 (over x).
Axes of the slice: x: 2, y: 2, z: 4, core: 2. Of those that a mesh axis runs over, the one named last changes fastest.
Arguments:
- facet_rows: bfloat16 [4, 2, 32, 4096], P('facet', None, 'team'), may hold values from -6 to 6
- sub_offsets: int32 [8, 2], replicated, may hold values from 0 to 4095
- facet_offsets: int32 [4, 2], replicated, may hold values from 0 to 4095
- aterm: bfloat16 [4, 2, 256, 256], P('facet'), may hold values from 0.29882812 to 3
- cells: int32 [4, 2, 4, 2, 256], P('facet', None, 'team'), may hold values from 0 to 1023
- observed: bfloat16 [4, 2, 4, 2, 256], P('facet', None, 'team'), may hold values from -6 to 6
- weights: bfloat16 [4, 2, 4, 256], P('facet', None, 'team'), may hold values from 0.29882812 to 3
- counts: int32 [4, 2, 4], replicated, may hold values from 1 to 256, as said below
Outputs:
- facet_update: float32 [4, 2, 32, 4096], P('facet', None, 'team', 'sub')
Inputs may be any that keep to these rules, and one draw needn't show every extreme that they name: Slots 0 to counts[a, b, t] - 1 are live. For every a and t one of the two subgrids with indices [a, 0] and [a, 1] has at most 64 live slots, and which of the two it is does not change with t.
All inputs are finite; a program needn't handle non-finite values.
Results may differ from a plain program's by a relative error of at most 0.019.
Values may be sent and summed in bfloat16 or wider, within the bound.
A program may use at most 64 MiB of HBM per device.

v0:
```python
import functools
import math

import jax
import jax.numpy as jnp
import ml_dtypes
import numpy as np
from jax import lax
from jax.experimental import pallas as pl
from jax.experimental.pallas import tpu as pltpu
from jax.sharding import PartitionSpec as P

M = 128
TWO_PI = 2.0 * math.pi
BF = jnp.bfloat16
F32 = jnp.float32
MESH = pl.DeviceIdType.MESH


def sincos(turns, period):
    shift = period.bit_length() - 3
    quad = (turns + (1 << (shift - 1))) >> shift
    t = (turns - (quad << shift)).astype(F32) * (TWO_PI / period)
    t2 = t * t
    s = t * (1.0 + t2 * (-1.0 / 6 + t2 * (1.0 / 120 + t2 * (-1.0 / 5040))))
    c = 1.0 + t2 * (-0.5 + t2 * (1.0 / 24 + t2 * (-1.0 / 720 + t2 * (1.0 / 40320))))
    odd = (quad & 1) != 0
    cos = jnp.where(odd, s, c)
    sin = jnp.where(odd, c, s)
    cos = jnp.where(((quad + 1) & 2) != 0, -cos, cos)
    sin = jnp.where((quad & 2) != 0, -sin, sin)
    return cos, sin


def mm(left, right):
    return jnp.dot(left, right, preferred_element_type=F32)


def mm_nt(left, right):
    return lax.dot_general(left, right, (((1,), (1,)), ((), ())), preferred_element_type=F32)


def cat(parts, axis):
    return jnp.concatenate(parts, axis)


def iota(shape, dim):
    return lax.broadcasted_iota(jnp.int32, shape, dim)


def body(
    dims,
    sub_off, fac_off, counts, rows, aterm, cells, observed, weights, table, kk, kt, kb,
    out,
    phi_c, phi_s, x_buf, spec_out, got1, fold_out, got2, fold3, got3,
    send1, recv1, send2, recv2, send3, recv3,
):
    nf, nt, nb, length, size, rdev = dims
    rall = rdev * nt
    n = nf * nt
    slots = cells.shape[-1]
    period = 4 * size
    my_f = lax.axis_index("facet")
    my_t = lax.axis_index("team")
    my_b = lax.axis_index("sub")
    me = my_f * nt + my_t
    other = 1 - my_b

    def peer_of(k):
        peer = lax.rem(me + k, n)
        return peer, peer // nt, lax.rem(peer, nt)

    barrier = pltpu.get_barrier_semaphore()

    def greet(k, carry):
        _, pf, pt = peer_of(k)
        pl.semaphore_signal(
            barrier, inc=1, device_id={"facet": pf, "team": pt, "sub": my_b}, device_id_type=MESH
        )
        return carry

    lax.fori_loop(1, n, greet, 0)
    pl.semaphore_signal(
        barrier, inc=1, device_id={"facet": my_f, "team": my_t, "sub": other}, device_id_type=MESH
    )

    sub_row = iota((nb * nf, 1), 0)
    tune = jnp.zeros((nb * nf, 1), jnp.int32)
    for s in range(nf):
        tune = jnp.where(sub_row == s, sub_off[s * nb + my_b, 1], tune)
        tune = jnp.where(sub_row == nf + s, sub_off[s * nb + other, 1], tune)
    pc, ps = sincos(iota((nb * nf, length), 1) * tune, length)
    phi_c[...] = pc
    phi_s[...] = ps
    re = rows[0, 0].astype(F32)
    im = rows[0, 1].astype(F32)
    for a in range(nf):
        c = phi_c[a : a + 1, :]
        s = phi_s[a : a + 1, :]
        x_buf[a] = re * c + im * s
        x_buf[nf + a] = im * c - re * s
    x = x_buf[...].reshape(2 * nf * rdev, length).astype(BF)
    y = mm(x, table[...])
    h = nf * rdev
    spec = cat([y[:h, :M] - y[h:, M:], y[:h, M:] + y[h:, :M]], 1)
    spec_out[...] = spec.reshape(nf, rdev, 2 * M).astype(BF)

    pl.semaphore_wait(barrier, n)

    def copy1(k):
        peer, pf, pt = peer_of(k)
        return pltpu.make_async_remote_copy(
            src_ref=spec_out.at[pf],
            dst_ref=got1.at[me],
            send_sem=send1.at[k],
            recv_sem=recv1.at[me],
            device_id={"facet": pf, "team": pt, "sub": my_b},
            device_id_type=MESH,
        )

    def start1(k, carry):
        copy1(k).start()
        return carry

    lax.fori_loop(1, n, start1, 0)
    got1[me] = spec_out[my_f]

    shift_u = jnp.int32(0)
    shift_u = sub_off[my_f * nb + my_b, 0]
    step = length // rall
    scale_g = 1.0 / math.sqrt(rall * nf)
    lane = iota((1, n * rdev), 1)
    col_a = jnp.zeros((1, n * rdev), jnp.int32)
    row = iota((n * rdev, 1), 0)
    row_a = jnp.zeros((n * rdev, 1), jnp.int32)
    row_c = jnp.zeros((n * rdev, 1), jnp.int32)
    for f in range(nf):
        col_a = jnp.where(lane // rall == f, fac_off[f, 0], col_a)
        row_a = jnp.where(row // rall == f, fac_off[f, 0], row_a)
        row_c = jnp.where(row // rall == f, fac_off[f, 1], row_c)
    p0 = iota((M, n * rdev), 0)
    gc, gs = sincos(p0 * col_a - (p0 + shift_u) * (lane % rall * step), length)
    gc = (gc * scale_g).astype(BF)
    gs = (gs * scale_g).astype(BF)
    a_mat = mm(kt[...], cat([cat([gc, gs], 1), cat([-gs, gc], 1)], 0)).astype(BF)
    p1 = iota((n * rdev, M), 1)
    hc, hs = sincos(p1 * row_a - (p1 + shift_u) * (row % rall * step), length)
    at = mm(cat([hc * scale_g, hs * scale_g], 1).astype(BF), kk[...])
    ah = cat([at[:, :size], -at[:, size:]], 1).astype(BF)
    ec, es = sincos(p1 * row_c, length)
    own_scale = math.sqrt(length / M) / size
    own_c, own_s = sincos(iota((rdev, M), 1) * fac_off[my_f, 1], length)
    own_c = own_c * own_scale
    own_s = own_s * own_scale
    pair = cells[0, my_b, 0]
    index = iota((size, slots), 0)
    rc, rs = sincos(index * pair[0:1, :], period)
    rc = rc.astype(BF)
    rs = rs.astype(BF)
    cc, cs = sincos(index * pair[1:2, :], period)
    cc = cc.astype(BF)
    cs = cs.astype(BF)
    col_w = cat([cat([cc, -cs], 1), cat([cs, cc], 1)], 0)
    left = cat([rc, rs], 1)
    amap = aterm[0, my_b].astype(F32)
    amap = cat([amap, amap], 1)
    obs = observed[0, my_b, 0].astype(F32)
    live = iota((1, slots), 1) < counts[my_f, my_b, my_t]
    wt = jnp.where(live, weights[0, my_b].astype(F32), 0.0)

    def take1(k, carry):
        peer, _, _ = peer_of(k)
        pltpu.make_async_copy(got1.at[peer], got1.at[peer], recv1.at[peer]).wait()
        return carry

    lax.fori_loop(1, n, take1, 0)
    sp = got1[...].astype(F32).reshape(n * rdev, 2 * M)
    sr = sp[:, :M]
    si = sp[:, M:]
    turned = cat([sr * ec - si * es, sr * es + si * ec], 1).astype(BF)
    t = mm(turned, kk[...]).astype(BF)
    tr = t[:, :size]
    ti = t[:, size:]
    image = mm(a_mat, cat([t, cat([-ti, tr], 1)], 0))
    weighted = (amap * image).astype(BF)
    z = mm(weighted, col_w)
    zr = z[:, :slots]
    zi = z[:, slots:]
    rcf = rc.astype(F32)
    rsf = rs.astype(F32)
    pred_re = jnp.sum(rcf * zr + rsf * zi, 0, keepdims=True) * (1.0 / size)
    pred_im = jnp.sum(rcf * zi - rsf * zr, 0, keepdims=True) * (1.0 / size)
    res_re = wt * (obs[0:1, :] - pred_re)
    res_im = wt * (obs[1:2, :] - pred_im)
    ccf = cc.astype(F32)
    csf = cs.astype(F32)
    s_re = (res_re * ccf - res_im * csf).astype(BF)
    s_im = (res_re * csf + res_im * ccf).astype(BF)
    grid = mm_nt(left, cat([cat([s_re, -s_im], 1), cat([s_im, s_re], 1)], 0))
    v = (amap * grid).astype(BF)
    u = mm(v, kb[...]).astype(BF)
    ur = u[:, :M]
    ui = u[:, M:]
    part = mm(ah, cat([u, cat([-ui, ur], 1)], 0))
    fold_out[...] = part.reshape(n, rdev, 2 * M).astype(BF)

    def copy2(k):
        peer, pf, pt = peer_of(k)
        return pltpu.make_async_remote_copy(
            src_ref=fold_out.at[peer],
            dst_ref=got2.at[me],
            send_sem=send2.at[k],
            recv_sem=recv2.at[me],
            device_id={"facet": pf, "team": pt, "sub": my_b},
            device_id_type=MESH,
        )

    def start2(k, carry):
        copy2(k).start()
        return carry

    lax.fori_loop(1, n, start2, 0)
    got2[me] = fold_out[me]

    def take2(k, carry):
        peer, _, _ = peer_of(k)
        pltpu.make_async_copy(got2.at[peer], got2.at[peer], recv2.at[peer]).wait()
        return carry

    lax.fori_loop(1, n, take2, 0)
    parts = got2[...].astype(F32).reshape(nf, nt, rdev, 2 * M)
    folded = jnp.sum(parts, 1)
    fr = folded[:, :, :M]
    fi = folded[:, :, M:]
    oc = own_c[None]
    os_ = own_s[None]
    fold3[...] = cat([fr * oc + fi * os_, fi * oc - fr * os_], 2).astype(BF)
    copy3 = pltpu.make_async_remote_copy(
        src_ref=fold3,
        dst_ref=got3,
        send_sem=send3,
        recv_sem=recv3,
        device_id={"facet": my_f, "team": my_t, "sub": other},
        device_id_type=MESH,
    )
    copy3.start()
    half = length // nb
    base = pl.multiple_of(my_b * half, 128)
    back = table[pl.ds(base, half), :]

    def update(stack, first):
        stack = stack.astype(F32).reshape(nf * rdev, 2 * M)
        turned = cat([stack[:, M:], -stack[:, :M]], 1)
        pre = mm_nt(cat([stack, turned], 0).astype(BF), back)
        tot_re = tot_im = None
        for a in range(nf):
            c = phi_c[first + a : first + a + 1, pl.ds(base, half)]
            s = phi_s[first + a : first + a + 1, pl.ds(base, half)]
            pr = pre[a * rdev : (a + 1) * rdev]
            pi = pre[h + a * rdev : h + (a + 1) * rdev]
            add_re = pr * c - pi * s
            add_im = pi * c + pr * s
            tot_re = add_re if tot_re is None else tot_re + add_re
            tot_im = add_im if tot_im is None else tot_im + add_im
        return tot_re, tot_im

    own_re, own_im = update(fold3[...], 0)
    copy3.wait_recv()
    oth_re, oth_im = update(got3[...], nf)
    out[0, 0] = own_re + oth_re
    out[0, 1] = own_im + oth_im

    def finish(k, carry):
        copy1(k).wait_send()
        copy2(k).wait_send()
        return carry

    lax.fori_loop(1, n, finish, 0)
    copy3.wait_send()


def tables(length, size):
    turn = np.arange(length)[:, None] * np.arange(M)[None, :] % length
    angle = turn * (TWO_PI / length)
    forward = np.concatenate([np.cos(angle), -np.sin(angle)], 1) / math.sqrt(length)
    angle = (np.arange(M)[:, None] * np.arange(size)[None, :] % size) * (TWO_PI / size)
    kc = np.cos(angle) / math.sqrt(M)
    ks = np.sin(angle) / math.sqrt(M)
    kk = np.block([[kc, ks], [-ks, kc]])
    kt = np.concatenate([kc.T, ks.T], 1)
    kb = np.block([[kc.T, -ks.T], [ks.T, kc.T]])
    return [np.asarray(v, np.float32).astype(ml_dtypes.bfloat16) for v in (forward, kk, kt, kb)]


def local(facet_rows, sub_offsets, facet_offsets, aterm, cells, observed, weights, counts):
    nf = lax.axis_size("facet")
    nt = lax.axis_size("team")
    nb = lax.axis_size("sub")
    rdev, length = facet_rows.shape[2:]
    size = aterm.shape[-1]
    n = nf * nt
    dims = (nf, nt, nb, length, size, rdev)
    consts = [jnp.asarray(v) for v in tables(length, size)]
    vm = pl.BlockSpec(memory_space=pltpu.VMEM)
    sm = pl.BlockSpec(memory_space=pltpu.SMEM)
    dma = pltpu.SemaphoreType.DMA
    return pl.pallas_call(
        functools.partial(body, dims),
        out_shape=jax.ShapeDtypeStruct((1, 2, rdev, length // nb), F32),
        in_specs=[sm] * 3 + [vm] * 9,
        out_specs=vm,
        scratch_shapes=[
            pltpu.VMEM((nb * nf, length), F32),
            pltpu.VMEM((nb * nf, length), F32),
            pltpu.VMEM((2 * nf, rdev, length), F32),
            pltpu.VMEM((nf, rdev, 2 * M), BF),
            pltpu.VMEM((n, rdev, 2 * M), BF),
            pltpu.VMEM((n, rdev, 2 * M), BF),
            pltpu.VMEM((n, rdev, 2 * M), BF),
            pltpu.VMEM((nf, rdev, 2 * M), BF),
            pltpu.VMEM((nf, rdev, 2 * M), BF),
            dma((n,)), dma((n,)), dma((n,)), dma((n,)), dma, dma,
        ],
        compiler_params=pltpu.CompilerParams(collective_id=0, has_side_effects=True),
    )(sub_offsets, facet_offsets, counts, facet_rows, aterm, cells, observed, weights, *consts)


def solution(mesh):
    placed = (
        P("facet", None, "team", None),
        P(),
        P(),
        P("facet", None, None, None),
        P("facet", None, "team", None, None),
        P("facet", None, "team", None, None),
        P("facet", None, "team", None),
        P(),
    )
    return jax.shard_map(
        local,
        mesh=mesh,
        in_specs=placed,
        out_specs=P("facet", None, "team", "sub"),
        check_vma=False,
    )
```

profile of v0, /device:TPU:0, one launch (start us, length us, event | category | flops | bytes accessed | tf_op | source)
XLA Modules:
  0.0 28.5 jit_solution(13941639981115756782)
XLA Ops:
  0.0 1.3 %copy.14.fac_off = s32[4,2]{1,0:T(4,128)} copy(s32[4,2]{0,1:T(2,128)} %param.14) | data formatting | bytes 64 | tf_op args[2]
  1.3 1.3 %copy.15.weights = bf16[1,2,1,256]{3,2,1,0:T(2,128)(2,1)} copy(bf16[1,2,1,256]{3,1,2,0:T(2,128)(2,1)} %param.18) | data formatting | bytes 2048 | tf_op args[6]
  2.6 1.3 %copy.13.sub_off = s32[8,2]{1,0:T(8,128)} copy(s32[8,2]{0,1:T(2,128)} %param.13) | data formatting | bytes 128 | tf_op args[1]
  4.0 23.0 %shard_map.118 = f32[1,2,8,2048]{3,2,1,0:T(8,128)} custom-call(s32[8,2]{1,0:T(8,128)} %copy.13.sub_off, s32[4,2]{1,0:T(4,128)} %copy.14.fac_off, s32[4,2,4]{2,1,0:T(2,128)} %counts.1, bf16[1,2,8,4096]{3,2,1,0:T(8,128)(2,1)} %rows.1, bf16[1,2,256,256]{3,2,1,0:T(8,128)(2,1)} %aterm.1, s32[1,2,1,2,256]{4,3,2,1,0:T(2,128)} %cells.1, ...), custom_call_target="tpu_custom_call" | custom-call | tf_op jit(solution)/shard_map/pallas_call | solution.py:307
  27.0 1.6 %copy.17 = f32[1,2,8,2048]{3,2,1,0:T(8,128)} copy(f32[1,2,8,2048]{3,2,1,0:T(8,128)} %shard_map.118) | data formatting | bytes 262144
where the time goes:
time: 28.7 us; the launch traced here: 28.5 us
  Pallas kernels  23 us (80%)
  local copies, waits for them, and re-layouts  5.53 us (19%)
    pallas_call x1, Pallas kernels, local(): pl.pallas_call(functools.partial(body, dims), out_shape=jax.ShapeDtypeStr...  23 us
    unnamed x4, local copies, waits for them, and re-layouts  5.53 us

commit v1 on v0

--- a/solution.py
+++ b/solution.py
@@ -50,11 +50,16 @@
 
 def body(
     dims,
-    sub_off, fac_off, counts, rows, aterm, cells, observed, weights, table, kk, kt, kb,
-    out,
+    *refs,
+):
+    ins = refs[:12]
+    out = refs[12]
+    bufs = refs[13:25]
+    (
     phi_c, phi_s, x_buf, spec_out, got1, fold_out, got2, fold3, got3,
-    send1, recv1, send2, recv2, send3, recv3,
-):
+    send1, recv1, send2, recv2, send3, recv3, in_sem, out_buf, out_sem,
+    ) = refs[25:]
+    sub_off, fac_off, counts, rows, aterm, cells, observed, weights, table, kk, kt, kb = bufs
     nf, nt, nb, length, size, rdev = dims
     rall = rdev * nt
     n = nf * nt
@@ -84,14 +89,20 @@
         barrier, inc=1, device_id={"facet": my_f, "team": my_t, "sub": other}, device_id_type=MESH
     )
 
+    fetches = [pltpu.make_async_copy(ins[i], bufs[i], in_sem.at[i]) for i in range(12)]
+    for i in (0, 3, 8, 1, 5, 10, 9, 4, 2, 6, 7, 11):
+        fetches[i].start()
+    fetches[0].wait()
+
     sub_row = iota((nb * nf, 1), 0)
     tune = jnp.zeros((nb * nf, 1), jnp.int32)
     for s in range(nf):
-        tune = jnp.where(sub_row == s, sub_off[s * nb + my_b, 1], tune)
-        tune = jnp.where(sub_row == nf + s, sub_off[s * nb + other, 1], tune)
+        tune = jnp.where(sub_row == s, sub_off[1, s * nb + my_b], tune)
+        tune = jnp.where(sub_row == nf + s, sub_off[1, s * nb + other], tune)
     pc, ps = sincos(iota((nb * nf, length), 1) * tune, length)
     phi_c[...] = pc
     phi_s[...] = ps
+    fetches[3].wait()
     re = rows[0, 0].astype(F32)
     im = rows[0, 1].astype(F32)
     for a in range(nf):
@@ -100,6 +111,7 @@
         x_buf[a] = re * c + im * s
         x_buf[nf + a] = im * c - re * s
     x = x_buf[...].reshape(2 * nf * rdev, length).astype(BF)
+    fetches[8].wait()
     y = mm(x, table[...])
     h = nf * rdev
     spec = cat([y[:h, :M] - y[h:, M:], y[:h, M:] + y[h:, :M]], 1)
@@ -125,8 +137,9 @@
     lax.fori_loop(1, n, start1, 0)
     got1[me] = spec_out[my_f]
 
-    shift_u = jnp.int32(0)
-    shift_u = sub_off[my_f * nb + my_b, 0]
+    for i in (1, 5, 10, 9, 4, 2, 6, 7, 11):
+        fetches[i].wait()
+    shift_u = sub_off[0, my_f * nb + my_b]
     step = length // rall
     scale_g = 1.0 / math.sqrt(rall * nf)
     lane = iota((1, n * rdev), 1)
@@ -135,9 +148,9 @@
     row_a = jnp.zeros((n * rdev, 1), jnp.int32)
     row_c = jnp.zeros((n * rdev, 1), jnp.int32)
     for f in range(nf):
-        col_a = jnp.where(lane // rall == f, fac_off[f, 0], col_a)
-        row_a = jnp.where(row // rall == f, fac_off[f, 0], row_a)
-        row_c = jnp.where(row // rall == f, fac_off[f, 1], row_c)
+        col_a = jnp.where(lane // rall == f, fac_off[0, f], col_a)
+        row_a = jnp.where(row // rall == f, fac_off[0, f], row_a)
+        row_c = jnp.where(row // rall == f, fac_off[1, f], row_c)
     p0 = iota((M, n * rdev), 0)
     gc, gs = sincos(p0 * col_a - (p0 + shift_u) * (lane % rall * step), length)
     gc = (gc * scale_g).astype(BF)
@@ -149,7 +162,7 @@
     ah = cat([at[:, :size], -at[:, size:]], 1).astype(BF)
     ec, es = sincos(p1 * row_c, length)
     own_scale = math.sqrt(length / M) / size
-    own_c, own_s = sincos(iota((rdev, M), 1) * fac_off[my_f, 1], length)
+    own_c, own_s = sincos(iota((rdev, M), 1) * fac_off[1, my_f], length)
     own_c = own_c * own_scale
     own_s = own_s * own_scale
     pair = cells[0, my_b, 0]
@@ -166,7 +179,9 @@
     amap = cat([amap, amap], 1)
     obs = observed[0, my_b, 0].astype(F32)
     live = iota((1, slots), 1) < counts[my_f, my_b, my_t]
-    wt = jnp.where(live, weights[0, my_b].astype(F32), 0.0)
+    all_wt = weights[0, 0].astype(F32)
+    own_wt = jnp.where(my_b == 0, all_wt[0:1, :], all_wt[1:2, :])
+    wt = jnp.where(live, own_wt, 0.0)
 
     def take1(k, carry):
         peer, _, _ = peer_of(k)
@@ -267,8 +282,10 @@
     own_re, own_im = update(fold3[...], 0)
     copy3.wait_recv()
     oth_re, oth_im = update(got3[...], nf)
-    out[0, 0] = own_re + oth_re
-    out[0, 1] = own_im + oth_im
+    out_buf[0, 0] = own_re + oth_re
+    out_buf[0, 1] = own_im + oth_im
+    put = pltpu.make_async_copy(out_buf, out, out_sem)
+    put.start()
 
     def finish(k, carry):
         copy1(k).wait_send()
@@ -277,6 +294,7 @@
 
     lax.fori_loop(1, n, finish, 0)
     copy3.wait_send()
+    put.wait()
 
 
 def tables(length, size):
@@ -301,15 +319,20 @@
     n = nf * nt
     dims = (nf, nt, nb, length, size, rdev)
     consts = [jnp.asarray(v) for v in tables(length, size)]
-    vm = pl.BlockSpec(memory_space=pltpu.VMEM)
-    sm = pl.BlockSpec(memory_space=pltpu.SMEM)
+    hbm = pl.BlockSpec(memory_space=pltpu.HBM)
+    operands = [
+        sub_offsets.T, facet_offsets.T, counts, facet_rows, aterm, cells, observed,
+        weights.transpose(0, 2, 1, 3), *consts,
+    ]
     dma = pltpu.SemaphoreType.DMA
     return pl.pallas_call(
         functools.partial(body, dims),
         out_shape=jax.ShapeDtypeStruct((1, 2, rdev, length // nb), F32),
-        in_specs=[sm] * 3 + [vm] * 9,
-        out_specs=vm,
+        in_specs=[hbm] * 12,
+        out_specs=pl.BlockSpec(memory_space=pl.ANY),
         scratch_shapes=[
+            *[pltpu.SMEM(v.shape, v.dtype) for v in operands[:3]],
+            *[pltpu.VMEM(v.shape, v.dtype) for v in operands[3:]],
             pltpu.VMEM((nb * nf, length), F32),
             pltpu.VMEM((nb * nf, length), F32),
             pltpu.VMEM((2 * nf, rdev, length), F32),
@@ -319,10 +342,14 @@
             pltpu.VMEM((n, rdev, 2 * M), BF),
             pltpu.VMEM((nf, rdev, 2 * M), BF),
             pltpu.VMEM((nf, rdev, 2 * M), BF),
-            dma((n,)), dma((n,)), dma((n,)), dma((n,)), dma, dma,
+            dma((n,)), dma((n,)), dma((n,)), dma((n,)), dma, dma, dma((12,)),
+            pltpu.VMEM((1, 2, rdev, length // nb), F32),
+            dma,
         ],
-        compiler_params=pltpu.CompilerParams(collective_id=0, has_side_effects=True),
-    )(sub_offsets, facet_offsets, counts, facet_rows, aterm, cells, observed, weights, *consts)
+        compiler_params=pltpu.CompilerParams(
+            collective_id=0, has_side_effects=True
+        ),
+    )(*operands)
 
 
 def solution(mesh):

time: 28.7 us -> 22.7 us (0.79)
  local copies, waits for them, and re-layouts: 5.53 us -> 1.57 us
  Pallas kernels: 23 us -> 21 us
    unnamed x4 -> x1, local copies, waits for them, and re-layouts: 5.53 us -> 1.57 us
    pallas_call x1, Pallas kernels: 23 us -> 21 us  [local(): pl.pallas_call(functools.partial(body, dims), out_shape=jax.ShapeDtypeStr...]
where the time goes in v1:
time: 22.7 us; the launch traced here: 22.6 us
  Pallas kernels  21 us (93%)
  local copies, waits for them, and re-layouts  1.57 us (7%)
    pallas_call x1, Pallas kernels, local(): pl.pallas_call(functools.partial(body, dims), out_shape=jax.ShapeDtypeStr...  21 us
    unnamed x1, local copies, waits for them, and re-layouts  1.57 us

profile of v1, /device:TPU:0, one launch (start us, length us, event | category | flops | bytes accessed | tf_op | source)
XLA Modules:
  0.0 22.6 jit_solution(11819630111256717877)
XLA Ops:
  0.0 21.0 %shard_map.118 = f32[1,2,8,2048]{3,2,1,0:T(8,128)} custom-call(s32[2,8]{1,0:T(2,128)} %bitcast.3, s32[2,4]{1,0:T(2,128)} %bitcast.4, s32[4,2,4]{2,1,0:T(2,128)} %refs_2_.1, bf16[1,2,8,4096]{3,2,1,0:T(8,128)(2,1)} %refs_3_.1, bf16[1,2,256,256]{3,2,1,0:T(8,128)(2,1)} %refs_4_.1, s32[1,2,1,2,256]{4,3,2,1,0:T(2,128)} %refs_5_.1, ...), custom_call_target="tpu_custom_call" | custom-call | tf_op jit(solution)/shard_map/pallas_call | solution.py:328
  21.0 1.6 %copy.14 = f32[1,2,8,2048]{3,2,1,0:T(8,128)} copy(f32[1,2,8,2048]{3,2,1,0:T(8,128)} %shard_map.118) | data formatting | bytes 262144

commit v2 on v1

--- a/solution.py
+++ b/solution.py
@@ -57,7 +57,7 @@
     bufs = refs[13:25]
     (
     phi_c, phi_s, x_buf, spec_out, got1, fold_out, got2, fold3, got3,
-    send1, recv1, send2, recv2, send3, recv3, in_sem, out_buf, out_sem,
+    send1, recv1, send2, recv2, send3, recv3, in_sem,
     ) = refs[25:]
     sub_off, fac_off, counts, rows, aterm, cells, observed, weights, table, kk, kt, kb = bufs
     nf, nt, nb, length, size, rdev = dims
@@ -282,10 +282,8 @@
     own_re, own_im = update(fold3[...], 0)
     copy3.wait_recv()
     oth_re, oth_im = update(got3[...], nf)
-    out_buf[0, 0] = own_re + oth_re
-    out_buf[0, 1] = own_im + oth_im
-    put = pltpu.make_async_copy(out_buf, out, out_sem)
-    put.start()
+    out[0, 0] = own_re + oth_re
+    out[0, 1] = own_im + oth_im
 
     def finish(k, carry):
         copy1(k).wait_send()
@@ -294,7 +292,6 @@
 
     lax.fori_loop(1, n, finish, 0)
     copy3.wait_send()
-    put.wait()
 
 
 def tables(length, size):
@@ -327,9 +324,9 @@
     dma = pltpu.SemaphoreType.DMA
     return pl.pallas_call(
         functools.partial(body, dims),
-        out_shape=jax.ShapeDtypeStruct((1, 2, rdev, length // nb), F32),
+        out_shape=pltpu.VMEM((1, 2, rdev, length // nb), F32),
         in_specs=[hbm] * 12,
-        out_specs=pl.BlockSpec(memory_space=pl.ANY),
+        out_specs=pl.BlockSpec(memory_space=pltpu.VMEM),
         scratch_shapes=[
             *[pltpu.SMEM(v.shape, v.dtype) for v in operands[:3]],
             *[pltpu.VMEM(v.shape, v.dtype) for v in operands[3:]],
@@ -343,8 +340,6 @@
             pltpu.VMEM((nf, rdev, 2 * M), BF),
             pltpu.VMEM((nf, rdev, 2 * M), BF),
             dma((n,)), dma((n,)), dma((n,)), dma((n,)), dma, dma, dma((12,)),
-            pltpu.VMEM((1, 2, rdev, length // nb), F32),
-            dma,
         ],
         compiler_params=pltpu.CompilerParams(
             collective_id=0, has_side_effects=True

time: 22.7 us -> 21.3 us (0.938)
  local copies, waits for them, and re-layouts: 1.57 us -> 0.66 us
  Pallas kernels: 21 us -> 20.4 us
    unnamed x1, local copies, waits for them, and re-layouts: 1.57 us -> 0.66 us
    pallas_call x1, Pallas kernels: 21 us -> 20.4 us  [local(): pl.pallas_call(functools.partial(body, dims), out_shape=pltpu.VMEM((1, 2,...]
where the time goes in v2:
time: 21.3 us; the launch traced here: 21.1 us
  Pallas kernels  20.4 us (96%)
  local copies, waits for them, and re-layouts  0.66 us (3%)
    pallas_call x1, Pallas kernels, local(): pl.pallas_call(functools.partial(body, dims), out_shape=pltpu.VMEM((1, 2,...  20.4 us
    unnamed x1, local copies, waits for them, and re-layouts  0.66 us

profile of v2, /device:TPU:0, one launch (start us, length us, event | category | flops | bytes accessed | tf_op | source)
XLA Modules:
  0.0 21.1 jit_solution(6985322641680554234)
XLA Ops:
  0.0 20.4 %shard_map.118 = f32[1,2,8,2048]{3,2,1,0:T(8,128)S(1)} custom-call(s32[2,8]{1,0:T(2,128)} %bitcast.3, s32[2,4]{1,0:T(2,128)} %bitcast.4, s32[4,2,4]{2,1,0:T(2,128)} %refs_2_.1, bf16[1,2,8,4096]{3,2,1,0:T(8,128)(2,1)} %refs_3_.1, bf16[1,2,256,256]{3,2,1,0:T(8,128)(2,1)} %refs_4_.1, s32[1,2,1,2,256]{4,3,2,1,0:T(2,128)} %refs_5_.1, ...), custom_call_target="tpu_custom_call" | custom-call | tf_op jit(solution)/shard_map/pallas_call | solution.py:325
  20.4 0.7 %copy.14 = f32[1,2,8,2048]{3,2,1,0:T(8,128)} copy(f32[1,2,8,2048]{3,2,1,0:T(8,128)S(1)} %shard_map.118) | data formatting | bytes 262144

commit v3 on v2

--- a/solution.py
+++ b/solution.py
@@ -56,8 +56,8 @@
     out = refs[12]
     bufs = refs[13:25]
     (
-    phi_c, phi_s, x_buf, spec_out, got1, fold_out, got2, fold3, got3,
-    send1, recv1, send2, recv2, send3, recv3, in_sem,
+    phi_c, phi_s, x_buf, spec_out, got1, fold_out, got2,
+    send1, recv1, send2, recv2, in_sem,
     ) = refs[25:]
     sub_off, fac_off, counts, rows, aterm, cells, observed, weights, table, kk, kt, kb = bufs
     nf, nt, nb, length, size, rdev = dims
@@ -219,52 +219,48 @@
     part = mm(ah, cat([u, cat([-ui, ur], 1)], 0))
     fold_out[...] = part.reshape(n, rdev, 2 * M).astype(BF)
 
-    def copy2(k):
+    def copy2(k, far):
         peer, pf, pt = peer_of(k)
         return pltpu.make_async_remote_copy(
             src_ref=fold_out.at[peer],
-            dst_ref=got2.at[me],
-            send_sem=send2.at[k],
-            recv_sem=recv2.at[me],
-            device_id={"facet": pf, "team": pt, "sub": my_b},
+            dst_ref=got2.at[far, me],
+            send_sem=send2.at[far, k],
+            recv_sem=recv2.at[far, me],
+            device_id={"facet": pf, "team": pt, "sub": other if far else my_b},
             device_id_type=MESH,
         )
 
     def start2(k, carry):
-        copy2(k).start()
-        return carry
-
+        copy2(k, 1).start()
+        copy2(k, 0).start()
+        return carry
+
+    copy2(0, 1).start()
     lax.fori_loop(1, n, start2, 0)
-    got2[me] = fold_out[me]
-
-    def take2(k, carry):
-        peer, _, _ = peer_of(k)
-        pltpu.make_async_copy(got2.at[peer], got2.at[peer], recv2.at[peer]).wait()
-        return carry
-
-    lax.fori_loop(1, n, take2, 0)
-    parts = got2[...].astype(F32).reshape(nf, nt, rdev, 2 * M)
-    folded = jnp.sum(parts, 1)
-    fr = folded[:, :, :M]
-    fi = folded[:, :, M:]
-    oc = own_c[None]
-    os_ = own_s[None]
-    fold3[...] = cat([fr * oc + fi * os_, fi * oc - fr * os_], 2).astype(BF)
-    copy3 = pltpu.make_async_remote_copy(
-        src_ref=fold3,
-        dst_ref=got3,
-        send_sem=send3,
-        recv_sem=recv3,
-        device_id={"facet": my_f, "team": my_t, "sub": other},
-        device_id_type=MESH,
-    )
-    copy3.start()
+    got2[0, me] = fold_out[me]
+
+    def take2(far):
+        def step(k, carry):
+            peer, _, _ = peer_of(k)
+            slot = got2.at[far, peer]
+            pltpu.make_async_copy(slot, slot, recv2.at[far, peer]).wait()
+            return carry
+
+        lax.fori_loop(1 - far, n, step, 0)
+        parts = got2[far].astype(F32).reshape(nf, nt, rdev, 2 * M)
+        folded = jnp.sum(parts, 1)
+        fr = folded[:, :, :M]
+        fi = folded[:, :, M:]
+        oc = own_c[None]
+        os_ = own_s[None]
+        return cat([fr * oc + fi * os_, fi * oc - fr * os_], 2)
+
     half = length // nb
     base = pl.multiple_of(my_b * half, 128)
     back = table[pl.ds(base, half), :]
 
     def update(stack, first):
-        stack = stack.astype(F32).reshape(nf * rdev, 2 * M)
+        stack = stack.reshape(nf * rdev, 2 * M)
         turned = cat([stack[:, M:], -stack[:, :M]], 1)
         pre = mm_nt(cat([stack, turned], 0).astype(BF), back)
         tot_re = tot_im = None
@@ -279,19 +275,19 @@
             tot_im = add_im if tot_im is None else tot_im + add_im
         return tot_re, tot_im
 
-    own_re, own_im = update(fold3[...], 0)
-    copy3.wait_recv()
-    oth_re, oth_im = update(got3[...], nf)
+    own_re, own_im = update(take2(0), 0)
+    oth_re, oth_im = update(take2(1), nf)
     out[0, 0] = own_re + oth_re
     out[0, 1] = own_im + oth_im
 
     def finish(k, carry):
         copy1(k).wait_send()
-        copy2(k).wait_send()
+        copy2(k, 0).wait_send()
+        copy2(k, 1).wait_send()
         return carry
 
     lax.fori_loop(1, n, finish, 0)
-    copy3.wait_send()
+    copy2(0, 1).wait_send()
 
 
 def tables(length, size):
@@ -336,10 +332,8 @@
             pltpu.VMEM((nf, rdev, 2 * M), BF),
             pltpu.VMEM((n, rdev, 2 * M), BF),
             pltpu.VMEM((n, rdev, 2 * M), BF),
-            pltpu.VMEM((n, rdev, 2 * M), BF),
-            pltpu.VMEM((nf, rdev, 2 * M), BF),
-            pltpu.VMEM((nf, rdev, 2 * M), BF),
-            dma((n,)), dma((n,)), dma((n,)), dma((n,)), dma, dma, dma((12,)),
+            pltpu.VMEM((nb, n, rdev, 2 * M), BF),
+            dma((n,)), dma((n,)), dma((nb, n)), dma((nb, n)), dma((12,)),
         ],
         compiler_params=pltpu.CompilerParams(
             collective_id=0, has_side_effects=True

time: 21.3 us -> 19.7 us (0.925)
  Pallas kernels: 20.4 us -> 18.9 us
    pallas_call x1, Pallas kernels: 20.4 us -> 18.9 us  [local(): pl.pallas_call(functools.partial(body, dims), out_shape=pltpu.VMEM((1, 2,...]
where the time goes in v3:
time: 19.7 us; the launch traced here: 19.5 us
  Pallas kernels  18.9 us (96%)
  local copies, waits for them, and re-layouts  0.66 us (3%)
    pallas_call x1, Pallas kernels, local(): pl.pallas_call(functools.partial(body, dims), out_shape=pltpu.VMEM((1, 2,...  18.9 us
    unnamed x1, local copies, waits for them, and re-layouts  0.66 us

profile of v3, /device:TPU:0, one launch (start us, length us, event | category | flops | bytes accessed | tf_op | source)
XLA Modules:
  0.0 19.5 jit_solution(12976392606953504264)
XLA Ops:
  0.0 18.9 %shard_map.118 = f32[1,2,8,2048]{3,2,1,0:T(8,128)S(1)} custom-call(s32[2,8]{1,0:T(2,128)} %bitcast.3, s32[2,4]{1,0:T(2,128)} %bitcast.4, s32[4,2,4]{2,1,0:T(2,128)} %refs_2_.1, bf16[1,2,8,4096]{3,2,1,0:T(8,128)(2,1)} %refs_3_.1, bf16[1,2,256,256]{3,2,1,0:T(8,128)(2,1)} %refs_4_.1, s32[1,2,1,2,256]{4,3,2,1,0:T(2,128)} %refs_5_.1, ...), custom_call_target="tpu_custom_call" | custom-call | tf_op jit(solution)/shard_map/pallas_call | solution.py:321
  18.9 0.7 %copy.14 = f32[1,2,8,2048]{3,2,1,0:T(8,128)} copy(f32[1,2,8,2048]{3,2,1,0:T(8,128)S(1)} %shard_map.118) | data formatting | bytes 262144
